TPU v7x, 32 devices: a whole 2x2x4 slice. The times are simulated.
32 devices in a mesh: grp: 2 (over y), tgt: 4 (over z), src: 4 (over x, core).
Axes of the slice: x: 2, y: 2, z: 4, core: 2. Of those that a mesh axis runs over, the one named last changes fastest.
Arguments:
- target_rows: bfloat16 [2048, 4608], P(('grp', 'tgt', 'src')), parts along dimension 0, may hold values from -6 to 6
- target_pos: int32 [2048], P(('grp', 'tgt')), parts along dimension 0, may hold values from 0 to 255
- decoder_rows: bfloat16 [512, 4608], P(('grp', 'tgt', 'src')), parts along dimension 0, may hold values from -0.09375 to 0.09375
- source_pos: int32 [512], P('grp'), parts along dimension 0, may hold values from 0 to 255
- out_proj: bfloat16 [32, 4608, 128], P('src', 'tgt'), may hold values from -0.09375 to 0.09375
- value_proj: bfloat16 [16, 4608, 128], P('src'), may hold values from -1 to 1
- attention: bfloat16 [64, 256, 256], P(('grp', 'src'), 'tgt'), parts along dimension 0, may hold values from 0 to 1, as said below
- tile_pattern: int32 [8, 4], P('grp'), parts along dimension 0, may hold values from 0 to 1, as said below
Outputs:
- edges: bfloat16 [512, 1024], P(('grp', 'src'), 'tgt'), parts along dimension 0
There are 2 independent parts, one for each index of `grp`. A program takes and returns all parts, laid end to end along the dimension named above; an argument that names none is the same for every part. Nothing has to cross between parts.
Inputs may be any that keep to these rules, and one draw needn't show every extreme that they name: Each row attention[h, p, :] is a probability distribution over the keys 0 to p: zero beyond p, summing to one. tile_pattern[b, c] is 1 where the tile of edges between source block b and target block c is kept, else 0.
All inputs are finite; a program needn't handle non-finite values.
Results may differ from a plain program's by a relative error of at most 0.0057.
Values may be sent and summed in bfloat16 or wider, within the bound.
A program may use at most 64 MiB of HBM per device.

v0:
```python
import jax
import jax.numpy as jnp
from jax import lax
from jax.sharding import PartitionSpec as P


def passed_along(value, axis, steps):
    count = lax.axis_size(axis)
    pairs = [(source, (source + steps) % count) for source in range(count)]
    return lax.ppermute(value, axis, pairs)


def shards(
    target_rows, target_pos, decoder_rows, source_pos, out_proj, value_proj, attention, tile_pattern
):
    blocks = lax.axis_size("tgt")
    column = lax.axis_index("tgt")
    src_lane = lax.axis_index("src")
    full_targets, full_sources = (
        lax.all_gather(target_rows, "src", axis=0, tiled=True),
        lax.all_gather(decoder_rows, "src", axis=0, tiled=True),
    )
    tgt_dev = full_targets.shape[0]
    src_dev = full_sources.shape[0]
    sub_rows = decoder_rows.shape[0]
    heads_here = out_proj.shape[0]
    head_dim = out_proj.shape[2]
    groups_here = value_proj.shape[0]
    repeat = heads_here // groups_here
    read_sum = jnp.einsum(
        "td,hde->the",
        full_targets,
        lax.all_gather(out_proj, "tgt", axis=1, tiled=True),
        preferred_element_type=jnp.float32,
    )
    head_reads = read_sum.astype(jnp.bfloat16).reshape(tgt_dev, groups_here, repeat, head_dim)
    values = jnp.einsum("sd,gde->sge", full_sources, value_proj, preferred_element_type=jnp.float32)
    values = values.astype(jnp.bfloat16).reshape(src_dev, groups_here * head_dim)
    attn_table = lax.all_gather(attention, "tgt", axis=1, tiled=True)
    target_attn = jnp.take(attn_table, target_pos, axis=1)
    keyed_attn = jnp.transpose(target_attn, (0, 2, 1))

    def edge_tile(payload, block_index):
        decoder_part, value_part = payload
        key_positions = lax.dynamic_slice_in_dim(source_pos, block_index * src_dev, src_dev)
        weights = jnp.take(keyed_attn, key_positions, axis=1).astype(jnp.float32)
        scores = jnp.einsum(
            "sgd,tgrd->grst",
            value_part.reshape(src_dev, groups_here, head_dim),
            head_reads,
            preferred_element_type=jnp.float32,
        )
        scores = scores.reshape(heads_here, src_dev, tgt_dev)
        mixed_term = jnp.sum(weights * scores, axis=0)
        own_positions = lax.dynamic_slice_in_dim(key_positions, src_lane * sub_rows, sub_rows)
        same_place = (own_positions[:, None] == target_pos[None, :]).astype(jnp.float32)
        direct = (
            jnp.einsum("sd,td->st", decoder_part, full_targets, preferred_element_type=jnp.float32)
            * same_place
        )
        own_rows = lax.dynamic_slice_in_dim(mixed_term, src_lane * sub_rows, sub_rows, 0)
        return lax.dynamic_update_slice_in_dim(
            mixed_term, own_rows + direct, src_lane * sub_rows, 0
        )

    def place_tile(partial_value, payload, block_index):
        kept_flag = tile_pattern[block_index, column]
        piece_tile = edge_tile(payload, block_index) * kept_flag.astype(jnp.float32)
        return lax.dynamic_update_slice_in_dim(partial_value, piece_tile, block_index * src_dev, 0)

    own_block = (decoder_rows, values)
    partial_value = jnp.zeros((blocks * src_dev, tgt_dev), jnp.float32)
    partial_value = place_tile(partial_value, own_block, column)

    def cycle_turn(turn_index, state_carry):
        forward_block, backward_block, running = state_carry
        forward_block = passed_along((forward_block[0], forward_block[1]), "tgt", 1)
        backward_block = passed_along((backward_block[0], backward_block[1]), "tgt", -1)
        running = place_tile(running, forward_block, (column - turn_index) % blocks)
        running = place_tile(running, backward_block, (column + turn_index) % blocks)
        return (forward_block, backward_block, running)

    forward_block, backward_block, partial_value = lax.fori_loop(
        1, blocks // 2, cycle_turn, (own_block, own_block, partial_value)
    )
    forward_block = passed_along((forward_block[0], forward_block[1]), "tgt", 1)
    partial_value = place_tile(partial_value, forward_block, (column - blocks // 2) % blocks)
    summed = lax.psum_scatter(partial_value, "src", scatter_dimension=0, tiled=True)
    return summed.astype(jnp.bfloat16)


def solution(mesh):
    return jax.shard_map(
        shards,
        mesh=mesh,
        in_specs=(
            P(("grp", "tgt", "src"), None),
            P(("grp", "tgt")),
            P(("grp", "tgt", "src"), None),
            P("grp"),
            P("src", "tgt", None),
            P("src", None, None),
            P(("grp", "src"), "tgt", None),
            P("grp", None),
        ),
        out_specs=P(("grp", "src"), "tgt"),
        check_vma=False,
    )
```

profile of v0, /device:TPU:0, one launch (start us, length us, event | category | flops | bytes accessed | tf_op | source)
XLA Modules:
  0.0 277.3 jit_solution(18094460157816442848)
XLA Ops:
  6.5 1.9 copy.26
  8.5 0.7 all-gather.6.cloned.1.call-update
  9.2 0.7 all-gather.8.cloned.1.call-update
  10.0 5.1 %collective-permute-start.3 = (bf16[16,4608]{1,0:T(8,128)(2,1)S(1)}, bf16[16,4608]{1,0:T(8,128)(2,1)S(1)}, u32[]{:S(2)}, u32[]{:S(2)}) collective-permute-start(bf16[16,4608]{1,0:T(8,128)(2,1)S(1)} %copy-done.2), channel_id=1, source_target_pairs={{0,12},{4,0},{8,4},{12,8},{1,13},{5,1},{9,5},{13,9},{2,14},{6,2},{... | collective-permute-start | bytes 442376 | tf_op jit(solution)/shard_map/while/body/eval_jaxpr/ppermute | solution.py:10
  15.1 7.5 %all_gather.15 = bf16[64,4608]{1,0:T(8,128)(2,1)S(1)} all-gather(bf16[16,4608]{1,0:T(8,128)(2,1)S(1)} %copy-done.2), channel_id=1, replica_groups=mesh['grp'=2,'tgt'=4,'src'=4] {'src'}, dimensions={0}, use_global_device_ids=true | all-gather | bytes 737280 | tf_op jit(solution)/shard_map/all_gather | solution.py:21
  22.6 3.3 %convolution_convert_fusion = bf16[64,4,128]{2,0,1:T(8,128)(2,1)S(1)} fusion(bf16[4,4608,128]{2,1,0:T(8,128)(2,1)} %param.15, bf16[64,4608]{1,0:T(8,128)(2,1)S(1)} %all_gather.15), kind=kOutput, calls=%fused_computation.8 | convolution fusion | flops 302022656 | bytes 5373952 | tf_op jit(solution)/shard_map/sd,gde->sge/dot_general | solution.py:37
  26.0 3.9 %collective-permute-start.2 = (bf16[64,512]{1,0:T(8,128)(2,1)S(1)}, bf16[64,512]{1,0:T(8,128)(2,1)S(1)}, u32[]{:S(2)}, u32[]{:S(2)}) collective-permute-start(bf16[64,512]{1,0:T(8,128)(2,1)S(1)} %copy_bitcast_fusion), channel_id=1, source_target_pairs={{0,12},{4,0},{8,4},{12,8},{1,13},{5,1},{9,5},{13,9},{2,14},{6,2},{... | collective-permute-start | bytes 196616 | tf_op jit(solution)/shard_map/while/body/eval_jaxpr/ppermute | solution.py:10
  30.1 0.7 fusion.26
  33.4 4.4 %collective-permute-done = bf16[64,512]{1,0:T(8,128)(2,1)S(1)} collective-permute-done((bf16[64,512]{1,0:T(8,128)(2,1)S(1)}, bf16[64,512]{1,0:T(8,128)(2,1)S(1)}, u32[]{:S(2)}, u32[]{:S(2)}) %collective-permute-start) | collective-permute-done | bytes 65568 | tf_op jit(solution)/shard_map/while/body/eval_jaxpr/ppermute | solution.py:10
  37.8 1.1 collective-permute-start.4
  39.0 5.8 %collective-permute-done.4 = bf16[64,512]{1,0:T(8,128)(2,1)S(1)} collective-permute-done((bf16[64,512]{1,0:T(8,128)(2,1)S(1)}, bf16[64,512]{1,0:T(8,128)(2,1)S(1)}, u32[]{:S(2)}, u32[]{:S(2)}) %collective-permute-start.4) | collective-permute-done | bytes 65568 | tf_op jit(solution)/shard_map/ppermute | solution.py:10
  44.9 2.0 gather_fusion
  46.9 0.9 select_bitcast_fusion
  47.8 1.3 copy.27
  49.1 0.6 gather_fusion.4
  49.7 0.6 gather_fusion.3
  50.3 0.6 gather_fusion.2
  50.9 0.6 gather_fusion.1
  51.5 17.4 %all-gather.6.cloned.1.call-done = bf16[256,4608]{1,0:T(8,128)(2,1)} async-done(((bf16[64,4608]{1,0:T(8,128)(2,1)}), bf16[256,4608]{1,0:T(8,128)(2,1)}) %all-gather.6.cloned.1.call-update) | async-done | bytes 2359312 | tf_op jit(solution)/shard_map/all_gather | solution.py:20
  68.9 168.4 %all-gather.8.cloned.1.call-done = bf16[8,4608,128]{2,1,0:T(8,128)(2,1)} async-done(((bf16[8,1152,128]{2,1,0:T(8,128)(2,1)}), bf16[8,4608,128]{2,1,0:T(8,128)(2,1)}) %all-gather.8.cloned.1.call-update) | async-done | bytes 9437200 | tf_op jit(solution)/shard_map/all_gather | solution.py:33
  237.2 7.0 %fusion.2 = bf16[256,8,128]{2,0,1:T(8,128)(2,1)S(1)} fusion(bf16[8,4608,128]{2,1,0:T(8,128)(2,1)} %all-gather.8.cloned.1.call-done, bf16[256,4608]{1,0:T(8,128)(2,1)} %all-gather.6.cloned.1.call-done), kind=kOutput, calls=%fused_computation.7 | convolution fusion | flops 2416181248 | bytes 12320768 | tf_op jit(solution)/shard_map/td,hde->the/dot_general | solution.py:30
  245.5 0.4 fusion.16
  245.9 0.4 fusion.17
  246.3 0.7 fusion.12
  247.1 0.7 fusion.10
  247.9 0.4 fusion.15
  248.3 0.7 fusion.8
  249.1 0.4 fusion.14
  249.5 0.7 fusion.6
  250.3 0.7 copy-done.1
  251.0 18.4 %reduce-scatter.2.cloned.1.call-done = f32[64,256]{1,0:T(8,128)} async-done(((f32[256,256]{1,0:T(8,128)}), f32[64,256]{1,0:T(8,128)}) %reduce-scatter.2.cloned.1.call-update) | async-done | bytes 65552 | tf_op jit(solution)/shard_map/reduce_scatter | solution.py:88
  269.3 1.5 convert_element_type.69
  (46 shorter events, 1.9 us)
Async XLA Ops:
  6.5 3.4 %copy-start.2 = (bf16[16,4608]{1,0:T(8,128)(2,1)S(1)}, bf16[16,4608]{1,0:T(8,128)(2,1)}, u32[]{:S(2)}) copy-start(bf16[16,4608]{1,0:T(8,128)(2,1)} %param.12) | copy-start | bytes 442372
  6.5 38.4 %all-gather.4.cloned.1.call-start = ((), (), s32[]{:S(2)}) async-start(), calls=%async_computation.1 | async-start | bytes 1310720 | tf_op jit(solution)/shard_map/all_gather | solution.py:39
  8.4 60.4 %all-gather.6.cloned.1.call-start = ((), (), s32[]{:S(2)}) async-start(), calls=%async_computation.2 | async-start | bytes 2949120 | tf_op jit(solution)/shard_map/all_gather | solution.py:20
  9.2 228.1 %all-gather.8.cloned.1.call-start = ((), (), s32[]{:S(2)}) async-start(), calls=%async_computation.3 | async-start | bytes 11796480 | tf_op jit(solution)/shard_map/all_gather | solution.py:33
  9.9 259.4 %reduce-scatter.2.cloned.1.call-start = ((), (), s32[]{:S(2)}) async-start(), calls=%async_computation.4 | async-start | bytes 327680 | tf_op jit(solution)/shard_map/reduce_scatter | solution.py:88
  10.0 238.3 %collective-permute-start.3 = (bf16[16,4608]{1,0:T(8,128)(2,1)S(1)}, bf16[16,4608]{1,0:T(8,128)(2,1)S(1)}, u32[]{:S(2)}, u32[]{:S(2)}) collective-permute-start(bf16[16,4608]{1,0:T(8,128)(2,1)S(1)} %copy-done.2), channel_id=1, source_target_pairs={{0,12},{4,0},{8,4},{12,8},{1,13},{5,1},{9,5},{13,9},{2,14},{6,2},{... | collective-permute-start | bytes 442376 | tf_op jit(solution)/shard_map/while/body/eval_jaxpr/ppermute | solution.py:10
  15.1 29.7 %collective-permute-start.1 = (bf16[16,4608]{1,0:T(8,128)(2,1)S(1)}, bf16[16,4608]{1,0:T(8,128)(2,1)S(1)}, u32[]{:S(2)}, u32[]{:S(2)}) collective-permute-start(bf16[16,4608]{1,0:T(8,128)(2,1)S(1)} %copy-done.2), channel_id=1, source_target_pairs={{0,4},{4,8},{8,12},{12,0},{1,5},{5,9},{9,13},{13,1},{2,6},{6,10},{... | collective-permute-start | bytes 442376 | tf_op jit(solution)/shard_map/while/body/eval_jaxpr/ppermute | solution.py:10
  22.6 7.2 %copy-start.3 = (s32[256]{0:T(256)S(1)}, s32[256]{0:T(256)}, u32[]{:S(2)}) copy-start(s32[256]{0:T(256)} %param.11) | copy-start | bytes 3076
  22.6 7.3 %copy-start.4 = (s32[256]{0:T(256)S(1)}, s32[256]{0:T(256)}, u32[]{:S(2)}) copy-start(s32[256]{0:T(256)} %param.13) | copy-start | bytes 3076
  22.6 7.5 %copy-start.5 = (s32[4,4]{1,0:T(4,128)S(1)}, s32[4,4]{1,0:T(4,128)}, u32[]{:S(2)}) copy-start(s32[4,4]{1,0:T(4,128)} %param.17) | copy-start | bytes 196
  26.0 13.0 %collective-permute-start.2 = (bf16[64,512]{1,0:T(8,128)(2,1)S(1)}, bf16[64,512]{1,0:T(8,128)(2,1)S(1)}, u32[]{:S(2)}, u32[]{:S(2)}) collective-permute-start(bf16[64,512]{1,0:T(8,128)(2,1)S(1)} %copy_bitcast_fusion), channel_id=1, source_target_pairs={{0,12},{4,0},{8,4},{12,8},{1,13},{5,1},{9,5},{13,9},{2,14},{6,2},{... | collective-permute-start | bytes 196616 | tf_op jit(solution)/shard_map/while/body/eval_jaxpr/ppermute | solution.py:10
  29.8 7.9 %collective-permute-start = (bf16[64,512]{1,0:T(8,128)(2,1)S(1)}, bf16[64,512]{1,0:T(8,128)(2,1)S(1)}, u32[]{:S(2)}, u32[]{:S(2)}) collective-permute-start(bf16[64,512]{1,0:T(8,128)(2,1)S(1)} %copy_bitcast_fusion), channel_id=1, source_target_pairs={{0,4},{4,8},{8,12},{12,0},{1,5},{5,9},{9,13},{13,1},{2,6},{6,10},{... | collective-permute-start | bytes 196616 | tf_op jit(solution)/shard_map/while/body/eval_jaxpr/ppermute | solution.py:10
  37.8 7.0 %collective-permute-start.4 = (bf16[64,512]{1,0:T(8,128)(2,1)S(1)}, bf16[64,512]{1,0:T(8,128)(2,1)S(1)}, u32[]{:S(2)}, u32[]{:S(2)}) collective-permute-start(bf16[64,512]{1,0:T(8,128)(2,1)S(1)} %collective-permute-done), channel_id=1, source_target_pairs={{0,4},{4,8},{8,12},{12,0},{1,5},{5,9},{9,13},{13,1},{2,6},{6,10},{... | collective-permute-start | bytes 196616 | tf_op jit(solution)/shard_map/ppermute | solution.py:10
  44.8 204.7 %collective-permute-start.5 = (bf16[16,4608]{1,0:T(8,128)(2,1)S(1)}, bf16[16,4608]{1,0:T(8,128)(2,1)S(1)}, u32[]{:S(2)}, u32[]{:S(2)}) collective-permute-start(bf16[16,4608]{1,0:T(8,128)(2,1)S(1)} %collective-permute-done.1), channel_id=1, source_target_pairs={{0,4},{4,8},{8,12},{12,0},{1,5},{5,9},{9,13},{13,1},{2,6},{6,10},{... | collective-permute-start | bytes 442376 | tf_op jit(solution)/shard_map/ppermute | solution.py:10
  244.5 1.8 copy-start
  250.3 0.7 copy-start.1
Sparse Core Ops, SparseCore 0:
  8.9 33.7 all-gather.3
  44.2 24.5 all-gather.5
  70.4 166.7 all-gather.7
  251.1 18.2 reduce-scatter.1
where the time goes:
time: 278 us; the launch traced here: 277 us
  waiting for transfers between devices  216 us (78%)
  between operations  16 us (6%)
  matrix products  14.3 us (5%)
  starting transfers between devices  10.4 us (4%)
  local copies, waits for them, and re-layouts  9.07 us (3%)
  blocking collectives  7.51 us (3%)
  other arithmetic  4.37 us (2%)
    all_gather x1, waiting for transfers between devices, shards(): lax.all_gather(out_proj, 'tgt', axis=1, tiled=True)  168 us
    reduce_scatter x1, waiting for transfers between devices, shards(): lax.psum_scatter(partial_value, 'src', scatter_dimension=0, tiled=True)  18.4 us
    all_gather x1, waiting for transfers between devices, shards(): lax.all_gather(target_rows, 'src', axis=0, tiled=True)  17.4 us
    ppermute x6, starting transfers between devices, passed_along(): return lax.ppermute(value, axis, pairs)  10.2 us
    ppermute x6, waiting for transfers between devices, passed_along(): return lax.ppermute(value, axis, pairs)  10.2 us
    all_gather x1, blocking collectives, shards(): lax.all_gather(decoder_rows, 'src', axis=0, tiled=True)  7.51 us
    dot_general x1, matrix products, shards(): jnp.einsum('td,hde->the', full_targets, lax.all_gather(out_proj, 'tgt', a...  6.99 us
  transfers between devices with their start and end apart: 10, of which 5 were waited for; matrix products, arithmetic and copies ran while one was open for 8% of the time, Pallas kernels for 0%

commit v1 on v0

--- a/solution.py
+++ b/solution.py
@@ -1,6 +1,10 @@
+import functools
+
 import jax
 import jax.numpy as jnp
 from jax import lax
+from jax.experimental import pallas as pl
+from jax.experimental.pallas import tpu as pltpu
 from jax.sharding import PartitionSpec as P
 
 
@@ -10,7 +14,7 @@
     return lax.ppermute(value, axis, pairs)
 
 
-def shards(
+def gathered_shards(
     target_rows, target_pos, decoder_rows, source_pos, out_proj, value_proj, attention, tile_pattern
 ):
     blocks = lax.axis_size("tgt")
@@ -87,6 +91,367 @@
     partial_value = place_tile(partial_value, forward_block, (column - blocks // 2) % blocks)
     summed = lax.psum_scatter(partial_value, "src", scatter_dimension=0, tiled=True)
     return summed.astype(jnp.bfloat16)
+
+
+F32 = jnp.float32
+BF16 = jnp.bfloat16
+MESH = pl.DeviceIdType.MESH
+
+
+def dot(a, b):
+    return jnp.dot(a, b, preferred_element_type=F32)
+
+
+def dot_nt(a, b):
+    return lax.dot_general(a, b, (((1,), (1,)), ((), ())), preferred_element_type=F32)
+
+
+def edge_kernel(
+    nt, ns, tgt_ref, tpos_ref, dec_ref, scol_ref, srow_ref, oproj_hbm, vproj_hbm, attn_ref, pat_ref,
+    out_ref,
+    oproj, vproj, tslices, dslices, decfull, attn, tpos, values, reads, attn_n, onehot, edges,
+    core_in, x_out, x_in, z_out, z_in,
+    local_sem, zt_s, zt_r, zd_s, zd_r, zp_s, zp_r, ar_s, al_s, a_r, zv_s, zv_r,
+    xt_s, xt_r, ct_s, ct_r, xf_s, xf_r, cf_s, cf_r, ce_s, ce_r, xe_s, xe_r, ze_s, ze_r,
+):
+    c = lax.axis_index("tgt")
+    s = lax.axis_index("src")
+    nx = ns // 2
+    x = s // 2
+    core = s % 2
+    mate = x * 2 + 1 - core
+    rows, depth = tslices.shape[1] // ns, tslices.shape[2]
+    sub = dec_ref.shape[0]
+    heads = oproj.shape[0]
+    groups = vproj.shape[0]
+    block = sub * ns
+    queries = attn_ref.shape[1]
+    own = edges.shape[1] // ns
+
+    def zdev(k):
+        return lax.rem(c + k, nt)
+
+    def xsrc(dx):
+        return lax.rem(x + dx, nx) * 2 + core
+
+    sent = []
+
+    def send(src, dst, ssem, rsem, axis, index):
+        cp = pltpu.make_async_remote_copy(
+            src_ref=src, dst_ref=dst, send_sem=ssem, recv_sem=rsem,
+            device_id={axis: index}, device_id_type=MESH,
+        )
+        cp.start()
+        sent.append(cp)
+
+    def arrived(dst, rsem):
+        pltpu.make_async_remote_copy(
+            src_ref=dst, dst_ref=dst, send_sem=local_sem.at[0], recv_sem=rsem,
+            device_id={"src": mate}, device_id_type=MESH,
+        ).wait_recv()
+
+    barrier = pltpu.get_barrier_semaphore()
+    for k in range(1, nt):
+        pl.semaphore_signal(barrier, inc=1, device_id={"tgt": zdev(k)}, device_id_type=MESH)
+    for dx in range(1, nx):
+        pl.semaphore_signal(barrier, inc=1, device_id={"src": xsrc(dx)}, device_id_type=MESH)
+    pl.semaphore_signal(barrier, inc=1, device_id={"src": mate}, device_id_type=MESH)
+    fetch_v = pltpu.make_async_copy(vproj_hbm, vproj, local_sem.at[1])
+    fetch_o = pltpu.make_async_copy(oproj_hbm, oproj, local_sem.at[2])
+    fetch_v.start()
+    fetch_o.start()
+    pl.semaphore_wait(barrier, nt - 1 + nx - 1 + 1)
+
+    def cols(b):
+        return pl.ds(pl.multiple_of(b * depth, 128), depth)
+
+    def trow(lane):
+        return pl.ds(pl.multiple_of(lane * rows, rows), rows)
+
+    def drow(lane):
+        return pl.ds(pl.multiple_of(lane * sub, sub), sub)
+
+    def qrow(b):
+        return pl.ds(pl.multiple_of(b * queries, queries), queries)
+
+    def vrow(b):
+        return pl.ds(pl.multiple_of(b * block, block), block)
+
+    def erow(lane):
+        return pl.ds(pl.multiple_of(lane * own, own), own)
+
+    for dx in range(1, nx):
+        send(dec_ref, decfull.at[drow(s)], xf_s.at[dx], xf_r.at[x], "src", xsrc(dx))
+    send(dec_ref, decfull.at[drow(s)], cf_s.at[0], cf_r.at[x], "src", mate)
+    for k in range(1, nt):
+        b = zdev(k)
+        send(tgt_ref.at[:, cols(b)], tslices.at[c, trow(s)], zt_s.at[k], zt_r.at[c], "tgt", b)
+        send(dec_ref.at[:, cols(b)], dslices.at[drow(c)], zd_s.at[k], zd_r.at[c], "tgt", b)
+        send(tpos_ref, tpos.at[c], zp_s.at[k], zp_r.at[c], "tgt", b)
+    for dx in range(1, nx):
+        send(tgt_ref.at[:, cols(c)], tslices.at[c, trow(s)], xt_s.at[0, dx], xt_r.at[c, x], "src", xsrc(dx))
+    send(tgt_ref.at[:, cols(c)], tslices.at[c, trow(s)], ct_s.at[0, 0], ct_r.at[c, x], "src", mate)
+
+    def to_right(src, b):
+        return pltpu.make_async_remote_copy(
+            src_ref=src, dst_ref=attn.at[:, qrow(b), :], send_sem=ar_s.at[b], recv_sem=a_r.at[b],
+            device_id={"tgt": c + 1}, device_id_type=MESH,
+        )
+
+    def to_left(src, b):
+        return pltpu.make_async_remote_copy(
+            src_ref=src, dst_ref=attn.at[:, qrow(b), :], send_sem=al_s.at[b], recv_sem=a_r.at[b],
+            device_id={"tgt": c - 1}, device_id_type=MESH,
+        )
+
+    @pl.when(c + 1 < nt)
+    def _():
+        to_right(attn_ref, c).start()
+
+    @pl.when(c > 0)
+    def _():
+        to_left(attn_ref, c).start()
+
+    tslices[c, trow(s)] = tgt_ref[:, cols(c)]
+    dslices[drow(c)] = dec_ref[:, cols(c)]
+    decfull[drow(s)] = dec_ref[...]
+    tpos[c] = tpos_ref[...]
+    attn[:, qrow(c), :] = attn_ref[...]
+
+    for dx in range(1, nx):
+        y = xsrc(dx)
+        arrived(decfull.at[drow(y)], xf_r.at[lax.rem(x + dx, nx)])
+        send(decfull.at[drow(y)], decfull.at[drow(y)], cf_s.at[dx], cf_r.at[lax.rem(x + dx, nx)], "src", mate)
+    for dx in range(nx):
+        z = lax.rem(x + dx, nx)
+        arrived(decfull.at[drow(z * 2 + 1 - core)], cf_r.at[z])
+    fetch_v.wait()
+
+    @pl.loop(0, groups)
+    def _(g):
+        values[g, vrow(c)] = dot(decfull[...], vproj[g]).astype(BF16)
+
+    fetch_o.wait()
+
+    def pass_rows(k):
+        b = zdev(nt - k)
+        arrived(tslices.at[b, trow(s)], zt_r.at[b])
+        for dx in range(1, nx):
+            send(tslices.at[b, trow(s)], tslices.at[b, trow(s)], xt_s.at[k, dx], xt_r.at[b, x], "src", xsrc(dx))
+        send(tslices.at[b, trow(s)], tslices.at[b, trow(s)], ct_s.at[k, 0], ct_r.at[b, x], "src", mate)
+
+    def pass_over(k):
+        b = zdev(nt - k) if k else c
+        for dx in range(1, nx):
+            z = lax.rem(x + dx, nx)
+            y = z * 2 + core
+            arrived(tslices.at[b, trow(y)], xt_r.at[b, z])
+            send(tslices.at[b, trow(y)], tslices.at[b, trow(y)], ct_s.at[k, dx], ct_r.at[b, z], "src", mate)
+
+    def read_block(k):
+        b = zdev(nt - k) if k else c
+        for dx in range(nx):
+            z = lax.rem(x + dx, nx)
+            arrived(tslices.at[b, trow(z * 2 + 1 - core)], ct_r.at[b, z])
+
+        @pl.loop(0, heads)
+        def _(h):
+            reads[b, h] = dot(tslices[b], oproj[h]).astype(BF16)
+
+    def relay(k):
+        @pl.when(c - k >= 0)
+        def _():
+            b = c - k
+            arrived(attn.at[:, qrow(b), :], a_r.at[b])
+
+            @pl.when(c + 1 < nt)
+            def _():
+                to_right(attn.at[:, qrow(b), :], b).start()
+
+        @pl.when(c + k < nt)
+        def _():
+            b = c + k
+            arrived(attn.at[:, qrow(b), :], a_r.at[b])
+
+            @pl.when(c > 0)
+            def _():
+                to_left(attn.at[:, qrow(b), :], b).start()
+
+    for k in range(1, nt):
+        send(values.at[:, vrow(c), :], values.at[:, vrow(c), :], zv_s.at[k], zv_r.at[c], "tgt", zdev(k))
+    for k in range(1, nt):
+        pass_rows(k)
+        pass_over(k - 1)
+    relay(1)
+    read_block(0)
+    pass_over(nt - 1)
+    for k in range(1, nt):
+        if k > 1:
+            relay(k)
+        read_block(k)
+    for k in range(1, nt):
+        b = zdev(k)
+        arrived(dslices.at[drow(b)], zd_r.at[b])
+        arrived(tpos.at[b], zp_r.at[b])
+        arrived(values.at[:, vrow(b), :], zv_r.at[b])
+
+    total = scol_ref.shape[0]
+    keys = attn.shape[2]
+    pick = (scol_ref[...] == lax.broadcasted_iota(jnp.int32, (total, keys), 1)).astype(BF16)
+
+    @pl.loop(0, heads)
+    def _(h):
+        attn_n[h] = dot_nt(pick, attn[h]).astype(BF16)
+
+    targets = tpos.shape[2]
+
+    def tile(k):
+        b = zdev(k + 1)
+        here = tpos[b]
+        onehot[...] = (lax.broadcasted_iota(jnp.int32, (nt * queries, targets), 0) == here).astype(BF16)
+        edges[b] = jnp.zeros(edges.shape[1:], F32)
+
+        @pl.loop(0, heads)
+        def _(h):
+            weights = dot(attn_n[h], onehot[...])
+            scores = dot_nt(values[h // (heads // groups)], reads[b, h])
+            edges[b] += weights * scores
+
+        direct = dot_nt(dslices[...], tslices[b])
+        for p in range(nt):
+            at = pl.ds(pl.multiple_of(p * block + s * sub, sub), sub)
+            same = (scol_ref[at] == here).astype(F32)
+            edges[b, at] += direct[p * sub:(p + 1) * sub] * same
+        for z in range(nx):
+            y = z * 2 + 1 - core
+            send(edges.at[b, erow(y)], core_in.at[b, z], ce_s.at[k, z], ce_r.at[b, z], "src", mate)
+
+    def over_x(k):
+        b = zdev(k + 1)
+        for z in range(nx):
+            arrived(core_in.at[b, z], ce_r.at[b, z])
+        for dx in range(1, nx):
+            z = lax.rem(x + dx, nx)
+            x_out[b, dx] = (edges[b, erow(z * 2 + core)] + core_in[b, z]).astype(BF16)
+            send(x_out.at[b, dx], x_in.at[b, x], xe_s.at[k, dx], xe_r.at[b, x], "src", z * 2 + core)
+
+    def over_z(k):
+        b = zdev(k + 1)
+        mine = edges[b, erow(s)] + core_in[b, x]
+        for dx in range(1, nx):
+            z = lax.rem(x + dx, nx)
+            arrived(x_in.at[b, z], xe_r.at[b, z])
+            mine += x_in[b, z].astype(F32)
+        if k < nt - 1:
+            z_out[b] = mine.astype(BF16)
+            send(z_out.at[b], z_in.at[c], ze_s.at[k], ze_r.at[c], "tgt", b)
+        return mine
+
+    for k in range(nt + 2):
+        if k < nt:
+            tile(k)
+        if 0 <= k - 1 < nt:
+            over_x(k - 1)
+        if 0 <= k - 2 < nt:
+            mine = over_z(k - 2)
+    for k in range(1, nt):
+        b = zdev(k)
+        arrived(z_in.at[b], ze_r.at[b])
+        mine += z_in[b].astype(F32)
+    kept = pat_ref[(s * own) // block, c]
+    out_ref[...] = (mine * kept.astype(F32)).astype(BF16)
+
+    for cp in sent:
+        cp.wait_send()
+    for k in range(nt):
+        @pl.when((c - k >= 0) & (c + 1 < nt))
+        def _():
+            to_right(attn_ref, c - k).wait_send()
+
+        @pl.when((c + k < nt) & (c > 0))
+        def _():
+            to_left(attn_ref, c + k).wait_send()
+
+
+def resident_shards(
+    target_rows, target_pos, decoder_rows, source_pos, out_proj, value_proj, attention, tile_pattern
+):
+    nt, ns = lax.axis_size("tgt"), lax.axis_size("src")
+    rows = target_rows.shape[0]
+    sub, width = decoder_rows.shape
+    heads, depth, head_dim = out_proj.shape
+    groups = value_proj.shape[0]
+    _, queries, keys = attention.shape
+    total = source_pos.shape[0]
+    targets = target_pos.shape[0]
+    own = total // ns
+    nx = ns // 2
+    vmem = pl.BlockSpec(memory_space=pltpu.VMEM)
+    hbm = pl.BlockSpec(memory_space=pl.ANY)
+    sem = lambda *shape: pltpu.SemaphoreType.DMA(shape)
+    return pl.pallas_call(
+        functools.partial(edge_kernel, nt, ns),
+        out_shape=jax.ShapeDtypeStruct((own, targets), BF16),
+        in_specs=[vmem, vmem, vmem, vmem, vmem, hbm, hbm, vmem, pl.BlockSpec(memory_space=pltpu.SMEM)],
+        out_specs=vmem,
+        scratch_shapes=[
+            pltpu.VMEM(out_proj.shape, BF16),
+            pltpu.VMEM(value_proj.shape, BF16),
+            pltpu.VMEM((nt, ns * rows, depth), BF16),
+            pltpu.VMEM((nt * sub, depth), BF16),
+            pltpu.VMEM((ns * sub, width), BF16),
+            pltpu.VMEM((heads, nt * queries, keys), BF16),
+            pltpu.VMEM((nt, 1, targets), jnp.int32),
+            pltpu.VMEM((groups, total, head_dim), BF16),
+            pltpu.VMEM((nt, heads, targets, head_dim), BF16),
+            pltpu.VMEM((heads, total, nt * queries), BF16),
+            pltpu.VMEM((nt * queries, targets), BF16),
+            pltpu.VMEM((nt, total, targets), F32),
+            pltpu.VMEM((nt, nx, own, targets), F32),
+            pltpu.VMEM((nt, nx, own, targets), BF16),
+            pltpu.VMEM((nt, nx, own, targets), BF16),
+            pltpu.VMEM((nt, own, targets), BF16),
+            pltpu.VMEM((nt, own, targets), BF16),
+            sem(3),
+            sem(nt), sem(nt), sem(nt), sem(nt), sem(nt), sem(nt),
+            sem(nt), sem(nt), sem(nt), sem(nt), sem(nt),
+            sem(nt, nx), sem(nt, nx), sem(nt, nx), sem(nt, nx),
+            sem(nx), sem(nx), sem(nx), sem(nx),
+            sem(nt, nx), sem(nt, nx), sem(nt, nx), sem(nt, nx), sem(nt), sem(nt),
+        ],
+        compiler_params=pltpu.CompilerParams(
+            collective_id=0, has_side_effects=True, vmem_limit_bytes=60 * 1024 * 1024
+        ),
+    )(
+        target_rows, target_pos.reshape(1, targets), decoder_rows, source_pos.reshape(total, 1),
+        source_pos.reshape(1, total), out_proj, value_proj, attention, tile_pattern,
+    )
+
+
+def resident_bytes(nt, ns, width, heads, depth, groups, rows, total, targets):
+    weights = heads * depth * 128 + groups * width * 128
+    gathered = nt * ns * rows * depth + nt * heads * targets * 128
+    return 2 * (weights + gathered) + 4 * nt * total * targets * 2
+
+
+def shards(
+    target_rows, target_pos, decoder_rows, source_pos, out_proj, value_proj, attention, tile_pattern
+):
+    nt, ns = lax.axis_size("tgt"), lax.axis_size("src")
+    heads, depth, head_dim = out_proj.shape
+    need = resident_bytes(
+        nt, ns, target_rows.shape[1], heads, depth, value_proj.shape[0], target_rows.shape[0],
+        source_pos.shape[0], target_pos.shape[0],
+    )
+    fits = (
+        depth % 128 == 0 and head_dim == 128 and ns % 2 == 0 and nt > 1
+        and decoder_rows.shape[0] % 16 == 0 and attention.shape[1] % 16 == 0
+        and need < 40 * 1024 * 1024
+    )
+    plan = resident_shards if fits else gathered_shards
+    return plan(
+        target_rows, target_pos, decoder_rows, source_pos, out_proj, value_proj, attention, tile_pattern
+    )
 
 
 def solution(mesh):

time: 278 us -> 69.3 us (0.25)
  waiting for transfers between devices: 216 us -> 0 us
  Pallas kernels: 0 us -> 66.3 us
  between operations: 16 us -> 0.01 us
  matrix products: 14.3 us -> 0 us
  starting transfers between devices: 10.4 us -> 0 us
  blocking collectives: 7.51 us -> 0 us
  local copies, waits for them, and re-layouts: 9.07 us -> 2.83 us
  other arithmetic: 4.37 us -> 0 us
    all_gather x3 -> x0, waiting for transfers between devices: 186 us -> none  [the longest x1 168 us: shards(): lax.all_gather(out_proj, 'tgt', axis=1, tiled=True)]
    pallas_call x0 -> x1, Pallas kernels: none -> 66.3 us  [resident_shards(): pl.pallas_call(functools.partial(edge_kernel, nt, ns), out_shape=jax.Shap...]
    reduce_scatter x1 -> x0, waiting for transfers between devices: 18.4 us -> none  [shards(): lax.psum_scatter(partial_value, 'src', scatter_dimension=0, tiled=True)]
    dot_general x10 -> x0, matrix products: 14.3 us -> none  [the longest x1 6.99 us: shards(): jnp.einsum('td,hde->the', full_targets, lax.all_gather(out_proj, 'tgt', a...]
    ppermute x6 -> x0, starting transfers between devices: 10.2 us -> none  [passed_along(): return lax.ppermute(value, axis, pairs)]
    ppermute x6 -> x0, waiting for transfers between devices: 10.2 us -> none  [passed_along(): return lax.ppermute(value, axis, pairs)]
    all_gather x1 -> x0, blocking collectives: 7.51 us -> none  [shards(): lax.all_gather(decoder_rows, 'src', axis=0, tiled=True)]
    gather x5 -> x0, local copies, waits for them, and re-layouts: 4.36 us -> none  [the longest x4 2.38 us: edge_tile(): weights = jnp.take(keyed_attn, key_positions, axis=1).astype(jnp.float32)]
  transfers between devices with their start and end apart: 10 -> 0, of which waited for: 5 -> 0; matrix products, arithmetic and copies ran while one was open for 8% -> 0% of each run, Pallas kernels for 0% -> 0%
where the time goes in v1:
time: 69.3 us; the launch traced here: 69.1 us
  Pallas kernels  66.3 us (96%)
  local copies, waits for them, and re-layouts  2.83 us (4%)
    pallas_call x1, Pallas kernels, resident_shards(): pl.pallas_call(functools.partial(edge_kernel, nt, ns), out_shape=jax.Shap...  66.3 us
    reshape x1, local copies, waits for them, and re-layouts, resident_shards(): source_pos.reshape(total, 1)  1.45 us

profile of v1, /device:TPU:0, one launch (start us, length us, event | category | flops | bytes accessed | tf_op | source)
XLA Modules:
  0.0 69.1 jit_solution(13597714905090373538)
XLA Ops:
  0.0 1.5 %copy.9.scol_ref = s32[256,1]{1,0:T(8,128)} copy(s32[256,1]{0,1:T(1,128)} %bitcast.3) | data formatting | bytes 2048 | tf_op jit(solution)/shard_map/reshape | solution.py:426
  1.5 66.3 %shard_map.82 = bf16[64,256]{1,0:T(8,128)(2,1)} custom-call(bf16[64,4608]{1,0:T(8,128)(2,1)} %tgt_ref.1, s32[1,256]{1,0:T(1,128)} %bitcast.5, bf16[16,4608]{1,0:T(8,128)(2,1)} %dec_ref.1, s32[256,1]{1,0:T(8,128)} %copy.9.scol_ref, s32[1,256]{1,0:T(1,128)} %bitcast.4, bf16[8,1152,128]{2,1,0:T(8,128)(2,1)} %oproj_hbm.1, bf16[4,4608,128]{2,1,0:T(8,128)(2,1)} %vproj_hbm.1, ...), custom_call_target="tpu_custom_call" | custom-call | tf_op jit(solution)/shard_map/pallas_call | solution.py:392
  67.8 1.4 %copy.11 = bf16[64,256]{1,0:T(8,128)(2,1)} copy(bf16[64,256]{1,0:T(8,128)(2,1)} %shard_map.82) | data formatting | bytes 65536

commit v2 on v1

--- a/solution.py
+++ b/solution.py
@@ -107,11 +107,11 @@
 
 
 def edge_kernel(
-    nt, ns, tgt_ref, tpos_ref, dec_ref, scol_ref, srow_ref, oproj_hbm, vproj_hbm, attn_ref, pat_ref,
+    nt, ns, tgt_ref, tpos_ref, dec_ref, srow_ref, oproj_hbm, vproj_hbm, attn_ref, pat_ref,
     out_ref,
     oproj, vproj, tslices, dslices, decfull, attn, tpos, values, reads, attn_n, onehot, edges,
-    core_in, x_out, x_in, z_out, z_in,
-    local_sem, zt_s, zt_r, zd_s, zd_r, zp_s, zp_r, ar_s, al_s, a_r, zv_s, zv_r,
+    core_in, x_out, x_in, z_out, z_in, scol_ref,
+    local_sem, zt_s, zt_r, zd_s, zd_r, zp_s, zp_r, ar_s, al_s, a_r, vr_s, vl_s, v_r,
     xt_s, xt_r, ct_s, ct_r, xf_s, xf_r, cf_s, cf_r, ce_s, ce_r, xe_s, xe_r, ze_s, ze_r,
 ):
     c = lax.axis_index("tgt")
@@ -125,7 +125,9 @@
     heads = oproj.shape[0]
     groups = vproj.shape[0]
     block = sub * ns
-    queries = attn_ref.shape[1]
+    queries, keys = attn_ref.shape[1:]
+    targets = tpos.shape[2]
+    total = scol_ref.shape[0]
     own = edges.shape[1] // ns
 
     def zdev(k):
@@ -133,6 +135,9 @@
 
     def xsrc(dx):
         return lax.rem(x + dx, nx) * 2 + core
+
+    def xother(dx):
+        return lax.rem(x + dx, nx) * 2 + 1 - core
 
     sent = []
 
@@ -155,12 +160,13 @@
         pl.semaphore_signal(barrier, inc=1, device_id={"tgt": zdev(k)}, device_id_type=MESH)
     for dx in range(1, nx):
         pl.semaphore_signal(barrier, inc=1, device_id={"src": xsrc(dx)}, device_id_type=MESH)
+        pl.semaphore_signal(barrier, inc=1, device_id={"src": xother(dx)}, device_id_type=MESH)
     pl.semaphore_signal(barrier, inc=1, device_id={"src": mate}, device_id_type=MESH)
     fetch_v = pltpu.make_async_copy(vproj_hbm, vproj, local_sem.at[1])
     fetch_o = pltpu.make_async_copy(oproj_hbm, oproj, local_sem.at[2])
     fetch_v.start()
     fetch_o.start()
-    pl.semaphore_wait(barrier, nt - 1 + nx - 1 + 1)
+    pl.semaphore_wait(barrier, nt - 1 + ns - 1)
 
     def cols(b):
         return pl.ds(pl.multiple_of(b * depth, 128), depth)
@@ -183,35 +189,61 @@
     for dx in range(1, nx):
         send(dec_ref, decfull.at[drow(s)], xf_s.at[dx], xf_r.at[x], "src", xsrc(dx))
     send(dec_ref, decfull.at[drow(s)], cf_s.at[0], cf_r.at[x], "src", mate)
-    for k in range(1, nt):
+    def spread(k):
         b = zdev(k)
         send(tgt_ref.at[:, cols(b)], tslices.at[c, trow(s)], zt_s.at[k], zt_r.at[c], "tgt", b)
         send(dec_ref.at[:, cols(b)], dslices.at[drow(c)], zd_s.at[k], zd_r.at[c], "tgt", b)
         send(tpos_ref, tpos.at[c], zp_s.at[k], zp_r.at[c], "tgt", b)
+
     for dx in range(1, nx):
         send(tgt_ref.at[:, cols(c)], tslices.at[c, trow(s)], xt_s.at[0, dx], xt_r.at[c, x], "src", xsrc(dx))
     send(tgt_ref.at[:, cols(c)], tslices.at[c, trow(s)], ct_s.at[0, 0], ct_r.at[c, x], "src", mate)
 
-    def to_right(src, b):
+    half = keys // 2
+    lowest = half // queries if half % 128 == 0 else 0
+
+    def attn_copy(src, b, ssem, device, act):
+        @pl.when(b < lowest)
+        def _():
+            act(pltpu.make_async_remote_copy(
+                src_ref=src.at[:, :, pl.ds(0, half)], dst_ref=attn.at[:, qrow(b), pl.ds(0, half)],
+                send_sem=ssem.at[b], recv_sem=a_r.at[b],
+                device_id={"tgt": device}, device_id_type=MESH,
+            ))
+
+        @pl.when(b >= lowest)
+        def _():
+            act(pltpu.make_async_remote_copy(
+                src_ref=src, dst_ref=attn.at[:, qrow(b), :],
+                send_sem=ssem.at[b], recv_sem=a_r.at[b],
+                device_id={"tgt": device}, device_id_type=MESH,
+            ))
+
+    def value_copy(b, ssem, device):
         return pltpu.make_async_remote_copy(
-            src_ref=src, dst_ref=attn.at[:, qrow(b), :], send_sem=ar_s.at[b], recv_sem=a_r.at[b],
-            device_id={"tgt": c + 1}, device_id_type=MESH,
+            src_ref=values.at[:, vrow(b), :], dst_ref=values.at[:, vrow(b), :],
+            send_sem=ssem.at[b], recv_sem=v_r.at[b],
+            device_id={"tgt": device}, device_id_type=MESH,
         )
 
-    def to_left(src, b):
-        return pltpu.make_async_remote_copy(
-            src_ref=src, dst_ref=attn.at[:, qrow(b), :], send_sem=al_s.at[b], recv_sem=a_r.at[b],
-            device_id={"tgt": c - 1}, device_id_type=MESH,
-        )
+    start = lambda copy: copy.start()
+    wait_send = lambda copy: copy.wait_send()
+    wait_recv = lambda copy: copy.wait_recv()
 
     @pl.when(c + 1 < nt)
     def _():
-        to_right(attn_ref, c).start()
+        attn_copy(attn_ref, c, ar_s, c + 1, start)
 
     @pl.when(c > 0)
     def _():
-        to_left(attn_ref, c).start()
-
+        attn_copy(attn_ref, c, al_s, c - 1, start)
+
+    spread(1)
+    spread(2)
+
+    for b in range(lowest):
+        attn[:, b * queries:(b + 1) * queries, half:] = jnp.zeros((heads, queries, keys - half), BF16)
+    scol_ref[...] = jnp.transpose(jnp.broadcast_to(srow_ref[...], (128, total)))[:, :1]
     tslices[c, trow(s)] = tgt_ref[:, cols(c)]
     dslices[drow(c)] = dec_ref[:, cols(c)]
     decfull[drow(s)] = dec_ref[...]
@@ -231,6 +263,14 @@
     def _(g):
         values[g, vrow(c)] = dot(decfull[...], vproj[g]).astype(BF16)
 
+    @pl.when(c + 1 < nt)
+    def _():
+        value_copy(c, vr_s, c + 1).start()
+
+    @pl.when(c > 0)
+    def _():
+        value_copy(c, vl_s, c - 1).start()
+
     fetch_o.wait()
 
     def pass_rows(k):
@@ -258,101 +298,117 @@
         def _(h):
             reads[b, h] = dot(tslices[b], oproj[h]).astype(BF16)
 
-    def relay(k):
+    def relay(k, copy_in, copy_on):
         @pl.when(c - k >= 0)
         def _():
-            b = c - k
-            arrived(attn.at[:, qrow(b), :], a_r.at[b])
+            copy_in(c - k)
 
             @pl.when(c + 1 < nt)
             def _():
-                to_right(attn.at[:, qrow(b), :], b).start()
+                copy_on(c - k, 0)
 
         @pl.when(c + k < nt)
         def _():
-            b = c + k
-            arrived(attn.at[:, qrow(b), :], a_r.at[b])
+            copy_in(c + k)
 
             @pl.when(c > 0)
             def _():
-                to_left(attn.at[:, qrow(b), :], b).start()
-
-    for k in range(1, nt):
-        send(values.at[:, vrow(c), :], values.at[:, vrow(c), :], zv_s.at[k], zv_r.at[c], "tgt", zdev(k))
-    for k in range(1, nt):
-        pass_rows(k)
-        pass_over(k - 1)
-    relay(1)
-    read_block(0)
-    pass_over(nt - 1)
-    for k in range(1, nt):
-        if k > 1:
-            relay(k)
-        read_block(k)
-    for k in range(1, nt):
-        b = zdev(k)
-        arrived(dslices.at[drow(b)], zd_r.at[b])
-        arrived(tpos.at[b], zp_r.at[b])
-        arrived(values.at[:, vrow(b), :], zv_r.at[b])
-
-    total = scol_ref.shape[0]
-    keys = attn.shape[2]
-    pick = (scol_ref[...] == lax.broadcasted_iota(jnp.int32, (total, keys), 1)).astype(BF16)
-
-    @pl.loop(0, heads)
-    def _(h):
-        attn_n[h] = dot_nt(pick, attn[h]).astype(BF16)
-
-    targets = tpos.shape[2]
-
-    def tile(k):
-        b = zdev(k + 1)
+                copy_on(c + k, 1)
+
+    def attn_in(b):
+        attn_copy(attn.at[:, qrow(b), :], b, ar_s, c, wait_recv)
+
+    def attn_on(b, left):
+        attn_copy(attn.at[:, qrow(b), :], b, al_s if left else ar_s, c - 1 if left else c + 1, start)
+
+    def value_in(b):
+        value_copy(b, vr_s, c).wait_recv()
+
+    def value_on(b, left):
+        value_copy(b, vl_s if left else vr_s, c - 1 if left else c + 1).start()
+
+    def prepare(k):
+        b = zdev(nt - k) if k else c
+        if k:
+            arrived(dslices.at[drow(b)], zd_r.at[b])
+            arrived(tpos.at[b], zp_r.at[b])
+        onehot[b] = (
+            lax.broadcasted_iota(jnp.int32, (nt * queries, targets), 0) == tpos[b]
+        ).astype(BF16)
+        edges[b] = jnp.zeros(edges.shape[1:], F32)
+
+    def add_direct(b):
         here = tpos[b]
-        onehot[...] = (lax.broadcasted_iota(jnp.int32, (nt * queries, targets), 0) == here).astype(BF16)
-        edges[b] = jnp.zeros(edges.shape[1:], F32)
-
-        @pl.loop(0, heads)
-        def _(h):
-            weights = dot(attn_n[h], onehot[...])
-            scores = dot_nt(values[h // (heads // groups)], reads[b, h])
-            edges[b] += weights * scores
-
         direct = dot_nt(dslices[...], tslices[b])
         for p in range(nt):
             at = pl.ds(pl.multiple_of(p * block + s * sub, sub), sub)
             same = (scol_ref[at] == here).astype(F32)
             edges[b, at] += direct[p * sub:(p + 1) * sub] * same
-        for z in range(nx):
-            y = z * 2 + 1 - core
-            send(edges.at[b, erow(y)], core_in.at[b, z], ce_s.at[k, z], ce_r.at[b, z], "src", mate)
-
-    def over_x(k):
-        b = zdev(k + 1)
-        for z in range(nx):
-            arrived(core_in.at[b, z], ce_r.at[b, z])
+
+    def pick_keys():
+        pick = (scol_ref[...] == lax.broadcasted_iota(jnp.int32, (total, keys), 1)).astype(BF16)
+
+        @pl.loop(0, heads)
+        def _(h):
+            attn_n[h] = dot_nt(pick, attn[h]).astype(BF16)
+
+    def tile(k):
+        b = zdev(nt - 1 - k)
+        repeat = heads // groups
+
+        @pl.loop(0, groups)
+        def _(g):
+            terms = None
+            for r in range(repeat):
+                h = g * repeat + r
+                term = dot(attn_n[h], onehot[b]) * dot_nt(values[g], reads[b, h])
+                terms = term if terms is None else terms + term
+            edges[b] += terms
+
+        send(edges.at[b, erow(mate)], core_in.at[b], ce_s.at[k], ce_r.at[b], "src", mate)
         for dx in range(1, nx):
-            z = lax.rem(x + dx, nx)
-            x_out[b, dx] = (edges[b, erow(z * 2 + core)] + core_in[b, z]).astype(BF16)
-            send(x_out.at[b, dx], x_in.at[b, x], xe_s.at[k, dx], xe_r.at[b, x], "src", z * 2 + core)
+            for y in (xsrc(dx), xother(dx)):
+                x_out[b, y] = edges[b, erow(y)].astype(BF16)
+                send(x_out.at[b, y], x_in.at[b, s], xe_s.at[k, y], xe_r.at[b, s], "src", y)
 
     def over_z(k):
-        b = zdev(k + 1)
-        mine = edges[b, erow(s)] + core_in[b, x]
+        b = zdev(nt - 1 - k)
+        arrived(core_in.at[b], ce_r.at[b])
+        mine = edges[b, erow(s)] + core_in[b]
         for dx in range(1, nx):
-            z = lax.rem(x + dx, nx)
-            arrived(x_in.at[b, z], xe_r.at[b, z])
-            mine += x_in[b, z].astype(F32)
+            for y in (xsrc(dx), xother(dx)):
+                arrived(x_in.at[b, y], xe_r.at[b, y])
+                mine += x_in[b, y].astype(F32)
         if k < nt - 1:
             z_out[b] = mine.astype(BF16)
             send(z_out.at[b], z_in.at[c], ze_s.at[k], ze_r.at[c], "tgt", b)
         return mine
 
-    for k in range(nt + 2):
+    prepare(0)
+    for k in range(1, nt):
+        relay(k, attn_in, attn_on)
+        if k == 1:
+            for j in range(3, nt):
+                spread(j)
+        relay(k, value_in, value_on)
+        if k == nt - 1:
+            pick_keys()
+        pass_rows(k)
+        pass_over(k - 1)
+        prepare(k)
+        if k == 1:
+            read_block(0)
+    for k in range(1, nt + 2):
         if k < nt:
-            tile(k)
-        if 0 <= k - 1 < nt:
-            over_x(k - 1)
-        if 0 <= k - 2 < nt:
+            read_block(k)
+            add_direct(zdev(nt - k))
+            tile(k - 1)
+        if k == 1:
+            pass_over(nt - 1)
+        if k == nt:
+            add_direct(c)
+            tile(k - 1)
+        if k > 1:
             mine = over_z(k - 2)
     for k in range(1, nt):
         b = zdev(k)
@@ -366,11 +422,13 @@
     for k in range(nt):
         @pl.when((c - k >= 0) & (c + 1 < nt))
         def _():
-            to_right(attn_ref, c - k).wait_send()
+            attn_copy(attn_ref, c - k, ar_s, c + 1, wait_send)
+            value_copy(c - k, vr_s, c + 1).wait_send()
 
         @pl.when((c + k < nt) & (c > 0))
         def _():
-            to_left(attn_ref, c + k).wait_send()
+            attn_copy(attn_ref, c + k, al_s, c - 1, wait_send)
+            value_copy(c + k, vl_s, c - 1).wait_send()
 
 
 def resident_shards(
@@ -392,7 +450,7 @@
     return pl.pallas_call(
         functools.partial(edge_kernel, nt, ns),
         out_shape=jax.ShapeDtypeStruct((own, targets), BF16),
-        in_specs=[vmem, vmem, vmem, vmem, vmem, hbm, hbm, vmem, pl.BlockSpec(memory_space=pltpu.SMEM)],
+        in_specs=[vmem, vmem, vmem, vmem, hbm, hbm, vmem, pl.BlockSpec(memory_space=pltpu.SMEM)],
         out_specs=vmem,
         scratch_shapes=[
             pltpu.VMEM(out_proj.shape, BF16),
@@ -405,26 +463,27 @@
             pltpu.VMEM((groups, total, head_dim), BF16),
             pltpu.VMEM((nt, heads, targets, head_dim), BF16),
             pltpu.VMEM((heads, total, nt * queries), BF16),
-            pltpu.VMEM((nt * queries, targets), BF16),
+            pltpu.VMEM((nt, nt * queries, targets), BF16),
             pltpu.VMEM((nt, total, targets), F32),
-            pltpu.VMEM((nt, nx, own, targets), F32),
-            pltpu.VMEM((nt, nx, own, targets), BF16),
-            pltpu.VMEM((nt, nx, own, targets), BF16),
+            pltpu.VMEM((nt, own, targets), F32),
+            pltpu.VMEM((nt, ns, own, targets), BF16),
+            pltpu.VMEM((nt, ns, own, targets), BF16),
             pltpu.VMEM((nt, own, targets), BF16),
             pltpu.VMEM((nt, own, targets), BF16),
+            pltpu.VMEM((total, 1), jnp.int32),
             sem(3),
             sem(nt), sem(nt), sem(nt), sem(nt), sem(nt), sem(nt),
-            sem(nt), sem(nt), sem(nt), sem(nt), sem(nt),
+            sem(nt), sem(nt), sem(nt), sem(nt), sem(nt), sem(nt),
             sem(nt, nx), sem(nt, nx), sem(nt, nx), sem(nt, nx),
             sem(nx), sem(nx), sem(nx), sem(nx),
-            sem(nt, nx), sem(nt, nx), sem(nt, nx), sem(nt, nx), sem(nt), sem(nt),
+            sem(nt), sem(nt), sem(nt, ns), sem(nt, ns), sem(nt), sem(nt),
         ],
         compiler_params=pltpu.CompilerParams(
             collective_id=0, has_side_effects=True, vmem_limit_bytes=60 * 1024 * 1024
         ),
     )(
-        target_rows, target_pos.reshape(1, targets), decoder_rows, source_pos.reshape(total, 1),
-        source_pos.reshape(1, total), out_proj, value_proj, attention, tile_pattern,
+        target_rows, target_pos.reshape(1, targets), decoder_rows, source_pos.reshape(1, total),
+        out_proj, value_proj, attention, tile_pattern,
     )
 
 
@@ -444,7 +503,7 @@
         source_pos.shape[0], target_pos.shape[0],
     )
     fits = (
-        depth % 128 == 0 and head_dim == 128 and ns % 2 == 0 and nt > 1
+        depth % 128 == 0 and head_dim == 128 and ns % 2 == 0 and nt > 2
         and decoder_rows.shape[0] % 16 == 0 and attention.shape[1] % 16 == 0
         and need < 40 * 1024 * 1024
     )

time: 69.3 us -> 63.7 us (0.919)
  Pallas kernels: 66.3 us -> 62.1 us
  local copies, waits for them, and re-layouts: 2.83 us -> 1.38 us
    pallas_call x1, Pallas kernels: 66.3 us -> 62.1 us  [resident_shards(): pl.pallas_call(functools.partial(edge_kernel, nt, ns), out_shape=jax.Shap...]
    reshape x1 -> x0, local copies, waits for them, and re-layouts: 1.45 us -> none  [resident_shards(): source_pos.reshape(total, 1)]
where the time goes in v2:
time: 63.7 us; the launch traced here: 63.5 us
  Pallas kernels  62.1 us (97%)
  local copies, waits for them, and re-layouts  1.38 us (2%)
    pallas_call x1, Pallas kernels, resident_shards(): pl.pallas_call(functools.partial(edge_kernel, nt, ns), out_shape=jax.Shap...  62.1 us
    unnamed x1, local copies, waits for them, and re-layouts  1.38 us

profile of v2, /device:TPU:0, one launch (start us, length us, event | category | flops | bytes accessed | tf_op | source)
XLA Modules:
  0.0 63.5 jit_solution(2825436155714072756)
XLA Ops:
  0.0 62.1 %shard_map.82 = bf16[64,256]{1,0:T(8,128)(2,1)} custom-call(bf16[64,4608]{1,0:T(8,128)(2,1)} %tgt_ref.1, s32[1,256]{1,0:T(1,128)} %bitcast.2, bf16[16,4608]{1,0:T(8,128)(2,1)} %dec_ref.1, s32[1,256]{1,0:T(1,128)} %bitcast.3, bf16[8,1152,128]{2,1,0:T(8,128)(2,1)} %oproj_hbm.1, bf16[4,4608,128]{2,1,0:T(8,128)(2,1)} %vproj_hbm.1, bf16[8,64,256]{2,1,0:T(8,128)(2,1)} %attn_ref.1, ...), custom_call_target="tpu_custom_call" | custom-call | tf_op jit(solution)/shard_map/pallas_call | solution.py:450
  62.1 1.4 %copy.10 = bf16[64,256]{1,0:T(8,128)(2,1)} copy(bf16[64,256]{1,0:T(8,128)(2,1)} %shard_map.82) | data formatting | bytes 65536
